TPU v7x, 32 devices: a whole 2x2x4 slice. The times are simulated.
32 devices in a mesh: batch: 4 (over x, core), cache: 8 (over z, y).
Axes of the slice: x: 2, y: 2, z: 4, core: 2. Of those that a mesh axis runs over, the one named last changes fastest.
Arguments:
- hidden_in: bfloat16 [32, 4096], P('batch'), may hold values from -6 to 6
- attn_gain: bfloat16 [4096], replicated, may hold values from 0.25 to 1.75
- w_query: bfloat16 [4096, 4096], P(None, 'cache'), may hold values from -0.09375 to 0.09375
- w_key: bfloat16 [4096, 1024], P(None, 'cache'), may hold values from -0.09375 to 0.09375
- w_value: bfloat16 [4096, 1024], P(None, 'cache'), may hold values from -0.09375 to 0.09375
- key_cache: bfloat16 [32, 1024, 1024], P('batch', 'cache'), may hold values from -400 to 400, as said below
- value_cache: bfloat16 [32, 1024, 1024], P('batch', 'cache'), may hold values from -6 to 6
- write_pos: int32 [32], P('batch'), may hold values from 0 to 3071, as said below
- cache_len: int32 [32], P('batch'), may hold values from 0 to 1023, as said below
- w_out: bfloat16 [4096, 4096], P('cache'), may hold values from -0.125 to 0.125
- mlp_gain: bfloat16 [4096], replicated, may hold values from 0.25 to 1.75
- w_gate: bfloat16 [4096, 7168], P(None, 'cache'), may hold values from -0.09375 to 0.09375
- w_up: bfloat16 [4096, 7168], P(None, 'cache'), may hold values from -0.09375 to 0.09375
- w_down: bfloat16 [7168, 4096], P('cache'), may hold values from -0.09375 to 0.09375
Outputs:
- hidden_out: bfloat16 [32, 4096], P('batch', 'cache')
Inputs may be any that keep to these rules, and one draw needn't show every extreme that they name: `key_cache`: keys of earlier tokens are finite reals. `write_pos`: positions of the new tokens; the largest value occurs in every draw. cache_len never exceeds write_pos; both 0 and 1023 occur in every draw, and many sequences attend fewer than 1023 earlier tokens.
All inputs are finite; a program needn't handle non-finite values.
Results may differ from a plain program's by a relative error of at most 0.017.
Values may be sent and summed in bfloat16 or wider, within the bound.
A program may use at most 64 MiB of HBM per device.

v0:
```python
import jax
import jax.numpy as jnp
from jax import lax
from jax.sharding import PartitionSpec as P

HEADS = 32
KV_HEADS = 8
HEAD_DIM = 128


def combined_all(value, axis, join):
    pieces = jax.tree.map(lambda part: lax.all_gather(part, axis), value)
    head = jax.tree.map(lambda part: part[0], pieces)
    tail = jax.tree.map(lambda part: part[1:], pieces)
    running, _ = lax.scan(lambda running, piece: (join(running, piece), None), head, tail)
    return running


def rms_norm(values, gain):
    wide = values.astype(jnp.float32)
    spread = jnp.mean(wide * wide, axis=-1, keepdims=True)
    return (wide * lax.rsqrt(spread + 1e-05) * gain.astype(jnp.float32)).astype(jnp.bfloat16)


def rotate(heads, position):
    half = heads.shape[-1] // 2
    freq = 10000.0 ** (-(jnp.arange(half, dtype=jnp.float32) * 2.0 / heads.shape[-1]))
    angle = position.astype(jnp.float32)[:, None] * freq[None, :]
    cosine = jnp.cos(angle)[:, None, :]
    sine = jnp.sin(angle)[:, None, :]
    first = heads[..., :half]
    second = heads[..., half:]
    return jnp.concatenate(
        [first * cosine - second * sine, second * cosine + first * sine], axis=-1
    )


def per_device(
    hidden_in,
    attn_gain,
    w_query,
    w_key,
    w_value,
    key_cache,
    value_cache,
    write_pos,
    cache_len,
    w_out,
    mlp_gain,
    w_gate,
    w_up,
    w_down,
):
    seqs = hidden_in.shape[0]
    embedding_width = hidden_in.shape[1]
    ncache = lax.axis_size("cache")
    position_index = lax.axis_index("cache")
    slots_dev = key_cache.shape[1]
    window = slots_dev * ncache
    group = HEADS // KV_HEADS
    scale = 1.0 / HEAD_DIM**0.5
    feature_width = embedding_width // ncache
    normed = rms_norm(hidden_in, attn_gain)
    query_slice = jnp.dot(normed, w_query, preferred_element_type=jnp.float32).astype(jnp.bfloat16)
    key_part = jnp.dot(normed, w_key, preferred_element_type=jnp.float32).astype(jnp.bfloat16)
    value_part = jnp.dot(normed, w_value, preferred_element_type=jnp.float32).astype(jnp.bfloat16)
    query_raw, key_raw, value_new = (
        lax.all_gather(query_slice, "cache", axis=1, tiled=True),
        lax.all_gather(key_part, "cache", axis=1, tiled=True),
        lax.all_gather(value_part, "cache", axis=1, tiled=True),
    )
    query = rotate(query_raw.astype(jnp.float32).reshape(seqs, HEADS, HEAD_DIM), write_pos).astype(
        jnp.bfloat16
    )
    fresh_key_row = rotate(
        key_raw.astype(jnp.float32).reshape(seqs, KV_HEADS, HEAD_DIM), write_pos
    ).astype(jnp.bfloat16)
    value_heads = value_new.reshape(seqs, KV_HEADS, HEAD_DIM)
    slots = position_index * slots_dev + jnp.arange(slots_dev, dtype=jnp.int32)
    dist = (write_pos[:, None] - 1 - slots[None, :]) % window + 1
    valid = dist <= cache_len[:, None]
    owner = write_pos % window // slots_dev == position_index
    query_head_group = query.reshape(seqs, KV_HEADS, group, HEAD_DIM)
    keys = key_cache.reshape(seqs, slots_dev, KV_HEADS, HEAD_DIM)
    values = value_cache.reshape(seqs, slots_dev, KV_HEADS, HEAD_DIM)
    scores = (
        jnp.einsum("bkgd,bwkd->bkgw", query_head_group, keys, preferred_element_type=jnp.float32)
        * scale
    )
    own = (
        jnp.einsum(
            "vyjf,vyf->vyj", query_head_group, fresh_key_row, preferred_element_type=jnp.float32
        )
        * scale
    )
    scores = jnp.where(valid[:, None, None, :], scores, -1e30)
    own = jnp.where(owner[:, None, None], own, -1e30)
    top = jnp.maximum(jnp.max(scores, axis=-1), own)
    weights = jnp.where(valid[:, None, None, :], jnp.exp(scores - top[..., None]), 0.0)
    own_weight = jnp.where(owner[:, None, None], jnp.exp(own - top), 0.0)
    total = jnp.sum(weights, axis=-1) + own_weight
    own_low = lax.optimization_barrier(own_weight.astype(jnp.bfloat16)).astype(jnp.float32)
    reduced_total = jnp.einsum(
        "bkgw,bwkd->bkgd", weights.astype(jnp.bfloat16), values, preferred_element_type=jnp.float32
    )
    reduced_total = (
        reduced_total + own_low[..., None] * value_heads.astype(jnp.float32)[:, :, None, :]
    )
    top_flat = top.reshape(seqs, HEADS)
    total_flat = total.reshape(seqs, HEADS)
    summed_flat = reduced_total.reshape(seqs, HEADS, HEAD_DIM)

    def combine(first, second):
        top_a, total_a, sum_a = first
        top_b, total_b, sum_b = second
        larger = jnp.maximum(top_a, top_b)
        factor_a = jnp.exp(top_a - larger)
        factor_b = jnp.exp(top_b - larger)
        merged = sum_a * factor_a[..., None] + sum_b * factor_b[..., None]
        return (larger, total_a * factor_a + total_b * factor_b, merged)

    merged_top, merged_total, merged_sum = combined_all(
        (top_flat, total_flat, summed_flat), "cache", combine
    )
    attended_heads_joined = (
        (merged_sum / merged_total[..., None]).reshape(seqs, HEADS * HEAD_DIM).astype(jnp.bfloat16)
    )
    attended = lax.dynamic_slice_in_dim(
        attended_heads_joined, position_index * feature_width, feature_width, 1
    )
    projected = jnp.dot(attended, w_out, preferred_element_type=jnp.float32)
    projected_sum = lax.psum(projected.astype(jnp.bfloat16), "cache").astype(jnp.float32)
    mid = (hidden_in.astype(jnp.float32) + projected_sum).astype(jnp.bfloat16)
    normed_mid = rms_norm(mid, mlp_gain)
    mid_own = lax.dynamic_slice_in_dim(mid, position_index * feature_width, feature_width, 1)
    gate = jnp.dot(normed_mid, w_gate, preferred_element_type=jnp.float32)
    upper = jnp.dot(normed_mid, w_up, preferred_element_type=jnp.float32)
    act = (jax.nn.silu(gate) * upper).astype(jnp.bfloat16)
    down = jnp.dot(act, w_down, preferred_element_type=jnp.float32)
    down_own = lax.psum_scatter(
        down.astype(jnp.bfloat16), "cache", scatter_dimension=1, tiled=True
    ).astype(jnp.float32)
    return (mid_own.astype(jnp.float32) + down_own).astype(jnp.bfloat16)


def solution(mesh):
    in_specs = (
        P("batch", None),
        P(),
        P(None, "cache"),
        P(None, "cache"),
        P(None, "cache"),
        P("batch", "cache", None),
        P("batch", "cache", None),
        P("batch"),
        P("batch"),
        P("cache", None),
        P(),
        P(None, "cache"),
        P(None, "cache"),
        P("cache", None),
    )
    out_specs = P("batch", "cache")
    return jax.shard_map(
        per_device, mesh=mesh, in_specs=in_specs, out_specs=out_specs, check_vma=False
    )
```

profile of v0, /device:TPU:0, one launch (start us, length us, event | category | flops | bytes accessed | tf_op | source)
XLA Modules:
  0.0 322.8 jit_solution(18037857481685795102)
XLA Ops:
  6.6 0.8 convert_element_type.87
  7.4 1.0 fusion.22
  8.4 1.6 convolution_convert_fusion.4
  10.0 27.9 %all_gather.19 = bf16[8,1024]{1,0:T(8,128)(2,1)S(1)} all-gather(bf16[8,128]{1,0:T(8,128)(2,1)S(1)} %convolution_convert_fusion.4), channel_id=1, replica_groups=mesh['batch'=4,'cache'=8] {'cache'}, dimensions={1}, use_global_device_ids=true | all-gather | bytes 18432 | tf_op jit(solution)/shard_map/all_gather | solution.py:69
  37.9 0.7 fusion.62
  38.6 3.0 convolution_convert_fusion.2
  41.6 30.5 %all_gather.18 = bf16[8,4096]{1,0:T(8,128)(2,1)S(1)} all-gather(bf16[8,512]{1,0:T(8,128)(2,1)S(1)} %convolution_convert_fusion.2), channel_id=1, replica_groups=mesh['batch'=4,'cache'=8] {'cache'}, dimensions={1}, use_global_device_ids=true | all-gather | bytes 73728 | tf_op jit(solution)/shard_map/all_gather | solution.py:68
  72.2 0.1 multiply_cosine_fusion
  72.3 0.1 subtract_convert_fusion.1
  72.4 0.1 subtract_convert_fusion
  72.6 0.1 maximum_bitcast_fusion
  72.7 0.3 fusion.33
  73.0 0.1 fusion.48
  73.1 1.3 fusion.63
  74.4 0.1 fusion.35
  74.4 0.3 fusion.27
  74.7 0.1 fusion.55
  74.9 0.3 convolution_convert_fusion.3
  75.2 26.1 %all_gather.22 = bf16[8,1024]{1,0:T(8,128)(2,1)S(1)} all-gather(bf16[8,128]{1,0:T(8,128)(2,1)S(1)} %convolution_convert_fusion.3), channel_id=1, replica_groups=mesh['batch'=4,'cache'=8] {'cache'}, dimensions={1}, use_global_device_ids=true | all-gather | bytes 18432 | tf_op jit(solution)/shard_map/all_gather | solution.py:70
  101.3 1.4 fusion.15
  102.7 0.0 all-gather.2.cloned.1.call-update
  102.7 0.0 all-reduce.2.cloned.1.call-start
  102.8 0.1 copy.34
  102.9 0.1 copy.36
  103.0 0.1 copy.37
  103.1 30.9 %all_gather.21 = f32[8,8,32]{2,1,0:T(8,128)S(1)} all-gather(f32[1,8,32]{2,1,0:T(8,128)S(1)} %copy.37), channel_id=1, replica_groups=mesh['batch'=4,'cache'=8] {'cache'}, dimensions={0}, use_global_device_ids=true | all-gather | bytes 9216 | tf_op jit(solution)/shard_map/all_gather | solution.py:12
  134.0 0.1 copy.35
  134.0 30.6 %all_gather.20 = f32[8,8,32]{2,1,0:T(8,128)S(1)} all-gather(f32[1,8,32]{2,1,0:T(8,128)S(1)} %copy.35), channel_id=1, replica_groups=mesh['batch'=4,'cache'=8] {'cache'}, dimensions={0}, use_global_device_ids=true | all-gather | bytes 9216 | tf_op jit(solution)/shard_map/all_gather | solution.py:12
  164.7 0.0 all-gather.2.cloned.1.call-done
  164.7 1.2 slice.49
  165.9 0.9 slice_bitcast_fusion
  166.9 1.5 while.14
  166.9 0.2 fusion.76
  167.1 0.2 fusion.76
  167.3 0.2 fusion.76
  167.5 0.2 fusion.76
  167.7 0.2 fusion.76
  167.9 0.2 fusion.76
  168.1 0.2 fusion.76
  168.3 0.1 fusion.31
  168.5 3.5 %convolution_convert_fusion.1 = bf16[8,4096]{1,0:T(8,128)(2,1)} fusion(bf16[512,4096]{1,0:T(8,128)(2,1)} %param.25, bf16[8,4096]{1,0:T(8,128)(2,1)S(1)} %bitcast.80, s32[]{:T(128)S(6)} %select_n.47), kind=kOutput, calls=%fused_computation.9 | convolution fusion | flops 33587200 | bytes 4268036 | tf_op jit(solution)/shard_map/dot_general | solution.py:131
  172.0 0.0 reduce-scatter.2.cloned.1.call-start
  172.0 67.0 %all-reduce.2.cloned.1.call-done = bf16[8,4096]{1,0:T(8,128)(2,1)} async-done(((bf16[8,4096]{1,0:T(8,128)(2,1)}), bf16[8,4096]{1,0:T(8,128)(2,1)}) %all-reduce.2.cloned.1.call-update) | async-done | bytes 65552 | tf_op jit(solution)/shard_map/psum | solution.py:132
  239.1 1.0 fusion.19
  240.1 4.2 %fusion.44 = f32[8,896]{1,0:T(8,128)S(1)} fusion(bf16[4096,896]{1,0:T(8,128)(2,1)} %param.27, bf16[8,4096]{1,0:T(8,128)(2,1)S(1)} %get-tuple-element.71, f32[4096]{0:T(1024)S(1)} %convert_element_type.105, f32[8]{0:T(128)S(1)} %add_rsqrt_fusion), kind=kOutput, calls=%fused_computation.67 | convolution fusion | flops 58851328 | bytes 7450656 | tf_op jit(solution)/shard_map/dot_general | solution.py:136
  244.2 8.1 %convolution_convert_fusion = bf16[8,4096]{1,0:T(8,128)(2,1)} fusion(bf16[896,4096]{1,0:T(8,128)(2,1)} %param.29, bf16[4096,896]{1,0:T(8,128)(2,1)} %param.28, f32[8,896]{1,0:T(8,128)S(1)} %fusion.44, bf16[8,4096]{1,0:T(8,128)(2,1)S(1)} %get-tuple-element.71, f32[4096]{0:T(1024)S(1)} %convert_element_type.105, f32[8]{0:T(128)S(1)} %add_rsqrt_fusion), kind=kOutput, calls=%fused_computation.8 | convolution fusion | flops 117647360 | bytes 14856224 | tf_op jit(solution)/shard_map/dot_general | solution.py:139
  252.4 62.5 %reduce-scatter.2.cloned.1.call-done = bf16[8,512]{1,0:T(8,128)(2,1)} async-done(((bf16[8,4096]{1,0:T(8,128)(2,1)}), bf16[8,512]{1,0:T(8,128)(2,1)}) %reduce-scatter.2.cloned.1.call-update) | async-done | bytes 8208 | tf_op jit(solution)/shard_map/reduce_scatter | solution.py:140
  314.9 1.3 add_convert_fusion.2
  (42 shorter events, 0.4 us)
Async XLA Ops:
  6.5 66.5 %copy-start = (bf16[8,128,1024]{2,1,0:T(8,128)(2,1)S(1)}, bf16[8,128,1024]{2,1,0:T(8,128)(2,1)}, u32[]{:S(2)}) copy-start(bf16[8,128,1024]{2,1,0:T(8,128)(2,1)} %param.21) | copy-start | bytes 6291460
  6.5 66.0 %copy-start.6 = (s32[8]{0:T(128)S(1)}, s32[8]{0:T(128)}, u32[]{:S(2)}) copy-start(s32[8]{0:T(128)} %param.23) | copy-start | bytes 100
  6.5 66.4 %copy-start.4 = (s32[8]{0:T(128)S(1)}, s32[8]{0:T(128)}, u32[]{:S(2)}) copy-start(s32[8]{0:T(128)} %param.24) | copy-start | bytes 100
  6.5 158.1 %all-gather.2.cloned.1.call-start = ((), (), s32[]{:S(2)}) async-start(), calls=%async_computation.1 | async-start | bytes 1179648 | tf_op jit(solution)/shard_map/all_gather | solution.py:12
  38.6 36.2 %copy-start.1 = (bf16[8,4096]{1,0:T(8,128)(2,1)S(1)}, bf16[8,4096]{1,0:T(8,128)(2,1)}, u32[]{:S(2)}) copy-start(bf16[8,4096]{1,0:T(8,128)(2,1)} %param.16) | copy-start | bytes 196612
  38.6 36.2 %copy-start.2 = (bf16[4096,128]{1,0:T(8,128)(2,1)S(1)}, bf16[4096,128]{1,0:T(8,128)(2,1)}, u32[]{:S(2)}) copy-start(bf16[4096,128]{1,0:T(8,128)(2,1)} %param.20) | copy-start | bytes 3145732
  72.6 28.7 %copy-start.5 = (bf16[8,128,1024]{2,1,0:T(8,128)(2,1)S(1)}, bf16[8,128,1024]{2,1,0:T(8,128)(2,1)}, u32[]{:S(2)}) copy-start(bf16[8,128,1024]{2,1,0:T(8,128)(2,1)} %param.22) | copy-start | bytes 6291460
  102.7 136.4 %all-reduce.2.cloned.1.call-start = ((), (), s32[]{:S(2)}) async-start(), calls=%async_computation.2 | async-start | bytes 131072 | tf_op jit(solution)/shard_map/psum | solution.py:132
  164.6 7.4 %copy-start.3 = (bf16[4096]{0:T(1024)(128)(2,1)S(1)}, bf16[4096]{0:T(1024)(128)(2,1)}, u32[]{:S(2)}) copy-start(bf16[4096]{0:T(1024)(128)(2,1)} %param.26) | copy-start | bytes 24580
  172.0 143.0 %reduce-scatter.2.cloned.1.call-start = ((), (), s32[]{:S(2)}) async-start(), calls=%async_computation.3 | async-start | bytes 73728 | tf_op jit(solution)/shard_map/reduce_scatter | solution.py:140
Sparse Core Ops, SparseCore 0:
  102.8 38.3 all-gather.1
  172.1 66.9 all-reduce.1
  252.5 62.3 reduce-scatter.1
where the time goes:
time: 323 us
  blocking collectives  146 us (45%)
  waiting for transfers between devices  130 us (40%)
  matrix products  23.6 us (7%)
  between operations  13.3 us (4%)
  other arithmetic  7.25 us (2%)
    psum x1, waiting for transfers between devices, per_device(): lax.psum(projected.astype(jnp.bfloat16), 'cache').astype(jnp.float32)  67 us
    reduce_scatter x1, waiting for transfers between devices, per_device(): lax.psum_scatter(down.astype(jnp.bfloat16), 'cache', scatter_dimension=1,...  62.5 us
    all_gather x2, blocking collectives, combined_all(): pieces = jax.tree.map(lambda part: lax.all_gather(part, axis), value)  61.5 us
    all_gather x1, blocking collectives, per_device(): lax.all_gather(query_slice, 'cache', axis=1, tiled=True)  30.5 us
    all_gather x1, blocking collectives, per_device(): lax.all_gather(key_part, 'cache', axis=1, tiled=True)  27.9 us
    all_gather x1, blocking collectives, per_device(): lax.all_gather(value_part, 'cache', axis=1, tiled=True)  26.1 us
    dot_general x1, matrix products, per_device(): down = jnp.dot(act, w_down, preferred_element_type=jnp.float32)  8.13 us
  transfers between devices with their start and end apart: 3, of which 2 were waited for; matrix products, arithmetic and copies ran while one was open for 0% of the time, Pallas kernels for 0%

commit v1 on v0

--- a/solution.py
+++ b/solution.py
@@ -129,7 +129,9 @@
         attended_heads_joined, position_index * feature_width, feature_width, 1
     )
     projected = jnp.dot(attended, w_out, preferred_element_type=jnp.float32)
-    projected_sum = lax.psum(projected.astype(jnp.bfloat16), "cache").astype(jnp.float32)
+    projected_sum = jnp.sum(lax.all_gather(projected.astype(jnp.bfloat16), "cache"), axis=0).astype(
+        jnp.float32
+    )
     mid = (hidden_in.astype(jnp.float32) + projected_sum).astype(jnp.bfloat16)
     normed_mid = rms_norm(mid, mlp_gain)
     mid_own = lax.dynamic_slice_in_dim(mid, position_index * feature_width, feature_width, 1)

time: 323 us -> 284 us (0.88)
  waiting for transfers between devices: 130 us -> 60.4 us
  blocking collectives: 146 us -> 177 us
    psum x1 -> x0, waiting for transfers between devices: 67 us -> none  [per_device(): lax.psum(projected.astype(jnp.bfloat16), 'cache').astype(jnp.float32)]
    all_gather x0 -> x1, blocking collectives: none -> 31.3 us  [per_device(): lax.all_gather(projected.astype(jnp.bfloat16), 'cache')]
  transfers between devices with their start and end apart: 3 -> 2, of which waited for: 2 -> 1; matrix products, arithmetic and copies ran while one was open for 0% -> 0% of each run, Pallas kernels for 0% -> 0%
where the time goes in v1:
time: 284 us
  blocking collectives  177 us (62%)
  waiting for transfers between devices  60.4 us (21%)
  matrix products  22.9 us (8%)
  between operations  13.6 us (5%)
  other arithmetic  6.46 us (2%)
    all_gather x2, blocking collectives, combined_all(): pieces = jax.tree.map(lambda part: lax.all_gather(part, axis), value)  61.5 us
    reduce_scatter x1, waiting for transfers between devices, per_device(): lax.psum_scatter(down.astype(jnp.bfloat16), 'cache', scatter_dimension=1,...  60.3 us
    all_gather x1, blocking collectives, per_device(): lax.all_gather(projected.astype(jnp.bfloat16), 'cache')  31.3 us
    all_gather x1, blocking collectives, per_device(): lax.all_gather(query_slice, 'cache', axis=1, tiled=True)  30.5 us
    all_gather x1, blocking collectives, per_device(): lax.all_gather(key_part, 'cache', axis=1, tiled=True)  27.9 us
    all_gather x1, blocking collectives, per_device(): lax.all_gather(value_part, 'cache', axis=1, tiled=True)  26.1 us
    dot_general x1, matrix products, per_device(): down = jnp.dot(act, w_down, preferred_element_type=jnp.float32)  8.13 us
  transfers between devices with their start and end apart: 2, of which 1 were waited for; matrix products, arithmetic and copies ran while one was open for 0% of the time, Pallas kernels for 0%

profile of v1, /device:TPU:0, one launch (start us, length us, event | category | flops | bytes accessed | tf_op | source)
XLA Modules:
  0.0 283.6 jit_solution(3126488763599877186)
XLA Ops:
  6.6 0.8 convert_element_type.89
  7.4 1.0 fusion.22
  8.4 1.6 convolution_convert_fusion.4
  10.0 27.9 %all_gather.25 = bf16[8,1024]{1,0:T(8,128)(2,1)S(1)} all-gather(bf16[8,128]{1,0:T(8,128)(2,1)S(1)} %convolution_convert_fusion.4), channel_id=1, replica_groups=mesh['batch'=4,'cache'=8] {'cache'}, dimensions={1}, use_global_device_ids=true | all-gather | bytes 18432 | tf_op jit(solution)/shard_map/all_gather | solution.py:69
  37.9 0.7 fusion.62
  38.6 3.0 %convolution_convert_fusion.2 = bf16[8,512]{1,0:T(8,128)(2,1)S(1)} fusion(bf16[4096,512]{1,0:T(8,128)(2,1)} %param.18, bf16[8,4096]{1,0:T(8,128)(2,1)} %param.16, f32[4096]{0:T(1024)S(1)} %convert_element_type.89, f32[8]{0:T(128)S(1)} %add_rsqrt_fusion.1), kind=kOutput, calls=%fused_computation.21 | convolution fusion | flops 33689600 | bytes 4284448 | tf_op jit(solution)/shard_map/dot_general | solution.py:64
  41.6 30.5 %all_gather.24 = bf16[8,4096]{1,0:T(8,128)(2,1)S(1)} all-gather(bf16[8,512]{1,0:T(8,128)(2,1)S(1)} %convolution_convert_fusion.2), channel_id=1, replica_groups=mesh['batch'=4,'cache'=8] {'cache'}, dimensions={1}, use_global_device_ids=true | all-gather | bytes 73728 | tf_op jit(solution)/shard_map/all_gather | solution.py:68
  72.2 0.1 multiply_cosine_fusion
  72.3 0.1 subtract_convert_fusion.1
  72.4 0.1 subtract_convert_fusion
  72.6 0.1 maximum_bitcast_fusion
  72.7 0.3 fusion.33
  73.0 0.1 fusion.48
  73.1 1.3 fusion.63
  74.4 0.1 fusion.35
  74.5 0.3 fusion.27
  74.8 0.1 fusion.55
  74.9 0.3 convolution_convert_fusion.3
  75.2 26.1 %all_gather.28 = bf16[8,1024]{1,0:T(8,128)(2,1)S(1)} all-gather(bf16[8,128]{1,0:T(8,128)(2,1)S(1)} %convolution_convert_fusion.3), channel_id=1, replica_groups=mesh['batch'=4,'cache'=8] {'cache'}, dimensions={1}, use_global_device_ids=true | all-gather | bytes 18432 | tf_op jit(solution)/shard_map/all_gather | solution.py:70
  101.3 1.4 fusion.15
  102.7 0.0 all-gather.3.cloned.1.call-update
  102.7 0.0 reduce-scatter.2.cloned.1.call-start
  102.8 0.1 copy.34
  102.9 0.1 copy.36
  103.0 0.1 copy.37
  103.1 30.9 %all_gather.27 = f32[8,8,32]{2,1,0:T(8,128)S(1)} all-gather(f32[1,8,32]{2,1,0:T(8,128)S(1)} %copy.37), channel_id=1, replica_groups=mesh['batch'=4,'cache'=8] {'cache'}, dimensions={0}, use_global_device_ids=true | all-gather | bytes 9216 | tf_op jit(solution)/shard_map/all_gather | solution.py:12
  134.0 0.1 copy.35
  134.0 30.6 %all_gather.26 = f32[8,8,32]{2,1,0:T(8,128)S(1)} all-gather(f32[1,8,32]{2,1,0:T(8,128)S(1)} %copy.35), channel_id=1, replica_groups=mesh['batch'=4,'cache'=8] {'cache'}, dimensions={0}, use_global_device_ids=true | all-gather | bytes 9216 | tf_op jit(solution)/shard_map/all_gather | solution.py:12
  164.7 0.0 all-gather.3.cloned.1.call-done
  164.7 1.2 slice.49
  166.0 0.9 slice_bitcast_fusion
  166.9 1.4 while.14
  166.9 0.2 fusion.76
  167.1 0.2 fusion.76
  167.3 0.2 fusion.76
  167.5 0.2 fusion.76
  167.7 0.2 fusion.76
  167.9 0.2 fusion.76
  168.2 0.2 fusion.76
  168.3 0.1 fusion.31
  168.5 2.8 %convolution_convert_fusion.1 = bf16[8,4096]{1,0:T(8,128)(2,1)S(1)} fusion(bf16[512,4096]{1,0:T(8,128)(2,1)} %param.25, bf16[8,4096]{1,0:T(8,128)(2,1)S(1)} %bitcast.82, s32[]{:T(128)S(6)} %select_n.47), kind=kOutput, calls=%fused_computation.9 | convolution fusion | flops 33587200 | bytes 4268036 | tf_op jit(solution)/shard_map/dot_general | solution.py:131
  171.3 31.3 %all-gather = bf16[64,4096]{1,0:T(8,128)(2,1)S(1)} all-gather(bf16[8,4096]{1,0:T(8,128)(2,1)S(1)} %convolution_convert_fusion.1), channel_id=2, replica_groups=mesh['batch'=4,'cache'=8] {'cache'}, dimensions={0}, use_global_device_ids=true | all-gather | bytes 589824 | tf_op jit(solution)/shard_map/all_gather | solution.py:132
  202.6 0.1 bitcast_reduce_fusion
  202.7 0.1 fusion.19
  202.8 4.2 %fusion.44 = f32[8,896]{1,0:T(8,128)S(1)} fusion(bf16[4096,896]{1,0:T(8,128)(2,1)} %param.27, bf16[8,4096]{1,0:T(8,128)(2,1)S(1)} %get-tuple-element.71, f32[4096]{0:T(1024)S(1)} %convert_element_type.107, f32[8]{0:T(128)S(1)} %add_rsqrt_fusion), kind=kOutput, calls=%fused_computation.68 | convolution fusion | flops 58851328 | bytes 7450656 | tf_op jit(solution)/shard_map/dot_general | solution.py:138
  207.0 8.1 %convolution_convert_fusion = bf16[8,4096]{1,0:T(8,128)(2,1)} fusion(bf16[896,4096]{1,0:T(8,128)(2,1)} %param.29, bf16[4096,896]{1,0:T(8,128)(2,1)} %param.28, f32[8,896]{1,0:T(8,128)S(1)} %fusion.44, bf16[8,4096]{1,0:T(8,128)(2,1)S(1)} %get-tuple-element.71, f32[4096]{0:T(1024)S(1)} %convert_element_type.107, f32[8]{0:T(128)S(1)} %add_rsqrt_fusion), kind=kOutput, calls=%fused_computation.8 | convolution fusion | flops 117647360 | bytes 14856224 | tf_op jit(solution)/shard_map/dot_general | solution.py:141
  215.1 60.3 %reduce-scatter.2.cloned.1.call-done = bf16[8,512]{1,0:T(8,128)(2,1)} async-done(((bf16[8,4096]{1,0:T(8,128)(2,1)}), bf16[8,512]{1,0:T(8,128)(2,1)}) %reduce-scatter.2.cloned.1.call-update) | async-done | bytes 8208 | tf_op jit(solution)/shard_map/reduce_scatter | solution.py:142
  275.5 1.3 add_convert_fusion.2
  (41 shorter events, 0.3 us)
Async XLA Ops:
  6.5 66.5 %copy-start = (bf16[8,128,1024]{2,1,0:T(8,128)(2,1)S(1)}, bf16[8,128,1024]{2,1,0:T(8,128)(2,1)}, u32[]{:S(2)}) copy-start(bf16[8,128,1024]{2,1,0:T(8,128)(2,1)} %param.21) | copy-start | bytes 6291460
  6.5 66.0 %copy-start.6 = (s32[8]{0:T(128)S(1)}, s32[8]{0:T(128)}, u32[]{:S(2)}) copy-start(s32[8]{0:T(128)} %param.23) | copy-start | bytes 100
  6.5 66.4 %copy-start.4 = (s32[8]{0:T(128)S(1)}, s32[8]{0:T(128)}, u32[]{:S(2)}) copy-start(s32[8]{0:T(128)} %param.24) | copy-start | bytes 100
  6.5 158.2 %all-gather.3.cloned.1.call-start = ((), (), s32[]{:S(2)}) async-start(), calls=%async_computation.1 | async-start | bytes 1179648 | tf_op jit(solution)/shard_map/all_gather | solution.py:12
  38.6 36.2 %copy-start.1 = (bf16[8,4096]{1,0:T(8,128)(2,1)S(1)}, bf16[8,4096]{1,0:T(8,128)(2,1)}, u32[]{:S(2)}) copy-start(bf16[8,4096]{1,0:T(8,128)(2,1)} %param.16) | copy-start | bytes 196612
  38.6 36.2 %copy-start.2 = (bf16[4096,128]{1,0:T(8,128)(2,1)S(1)}, bf16[4096,128]{1,0:T(8,128)(2,1)}, u32[]{:S(2)}) copy-start(bf16[4096,128]{1,0:T(8,128)(2,1)} %param.20) | copy-start | bytes 3145732
  72.4 92.2 %copy-start.3 = (bf16[4096]{0:T(1024)(128)(2,1)S(1)}, bf16[4096]{0:T(1024)(128)(2,1)}, u32[]{:S(2)}) copy-start(bf16[4096]{0:T(1024)(128)(2,1)} %param.26) | copy-start | bytes 24580
  72.6 28.7 %copy-start.5 = (bf16[8,128,1024]{2,1,0:T(8,128)(2,1)S(1)}, bf16[8,128,1024]{2,1,0:T(8,128)(2,1)}, u32[]{:S(2)}) copy-start(bf16[8,128,1024]{2,1,0:T(8,128)(2,1)} %param.22) | copy-start | bytes 6291460
  102.7 172.7 %reduce-scatter.2.cloned.1.call-start = ((), (), s32[]{:S(2)}) async-start(), calls=%async_computation.2 | async-start | bytes 73728 | tf_op jit(solution)/shard_map/reduce_scatter | solution.py:142
Sparse Core Ops, SparseCore 0:
  102.8 38.3 all-gather.2
  215.3 60.1 reduce-scatter.1
